TPU v7x, 256 devices: a whole 4x4x8 slice. The times are simulated.
256 devices in a mesh: pipe: 8 (over x, z_lo), tensor: 4 (over y), expert: 8 (over z_hi, core).
Axes of the slice: x: 4, y: 4, z: 8 (z_hi: 4, z_lo: 2; z = z_hi * 2 + z_lo), core: 2. Of those that a mesh axis runs over, the one named last changes fastest.
Arguments:
- tokens: bfloat16 [2, 512, 4096], P(None, 'expert'), may hold values from -6 to 6
- gains: float32 [8, 4096], P('pipe'), may hold values from 0.1 to 1.9
- route_ids: int32 [8, 2, 512, 2], P('pipe', None, 'expert'), may hold values from 0 to 7, all different within a row
- route_weights: float32 [8, 2, 512, 2], P('pipe', None, 'expert'), may hold values from 0.2 to 1
- picks: int32 [8, 2, 8, 64], P('pipe', None, 'expert'), may hold values from 0 to 63, each once within a row
- w_gate: bfloat16 [8, 8, 4096, 1536], P('pipe', 'expert', None, 'tensor'), may hold values from -0.09375 to 0.09375
- w_up: bfloat16 [8, 8, 4096, 1536], P('pipe', 'expert', None, 'tensor'), may hold values from -0.09375 to 0.09375
- w_down: bfloat16 [8, 8, 1536, 4096], P('pipe', 'expert', 'tensor'), may hold values from -0.15625 to 0.15625
Outputs:
- streams: bfloat16 [8, 2, 512, 4096], P('pipe', None, 'expert', 'tensor')
Inputs may be any that keep to these rules, and one draw needn't show every extreme that they name: `route_ids`: each token names 2 different experts; every expert is named by some token. `picks`: for every layer, micro-batch and block of 64 tokens, a permutation of 0 to 63.
All inputs are finite; a program needn't handle non-finite values.
Results may differ from a plain program's by a relative error of at most 0.025.
Values may be sent and summed in bfloat16 or wider, within the bound.
A program may use at most 64 MiB of HBM per device.

v0:
```python
import jax
import jax.numpy as jnp
from jax import lax
from jax.sharding import PartitionSpec as P

epsilon = 1e-06


def from_everyone(value, axis):
    copies = jnp.broadcast_to(value, (lax.axis_size(axis), *value.shape))
    return lax.all_to_all(copies, axis, split_axis=0, concat_axis=0, tiled=True)


def joined_along(pieces, dim):
    pieces = jnp.moveaxis(pieces, 0, dim)
    shape = pieces.shape
    return pieces.reshape(*shape[:dim], shape[dim] * shape[dim + 1], *shape[dim + 2 :])


def gather_directly(value, axis, dim):
    pieces = from_everyone(value, axis)
    return joined_along(pieces, dim)


def cut_along(value, dim, count):
    before, after = (value.shape[:dim], value.shape[dim + 1 :])
    return jnp.moveaxis(value.reshape(*before, count, -1, *after), dim, 0)


def sum_at_owner(value, axis, dim):
    pieces = cut_along(value, dim, lax.axis_size(axis))
    arrived = lax.all_to_all(pieces, axis, split_axis=0, concat_axis=0, tiled=True)
    return arrived.astype(jnp.float32).sum(axis=0)


def passed_along(block, axis, distance):
    devices = range(lax.axis_size(axis))
    route = [(i - distance, i) for i in devices if i - distance in devices]
    return lax.ppermute(block, axis, route)


def local(tokens, gains, route_ids, route_weights, picks, w_gate, w_up, w_down):
    micro_count = tokens.shape[0]
    local_tokens = tokens.shape[1]
    model_width = tokens.shape[2]
    route_count = route_ids.shape[3]
    tensor_ranks = lax.axis_size("tensor")
    groups = lax.axis_size("expert")
    sections = lax.axis_size("pipe")
    quarter = local_tokens // tensor_ranks
    capacity = 4 * quarter * route_count // (3 * groups)
    slice_width = model_width // tensor_ranks
    my_section = lax.axis_index("pipe")
    my_rank = lax.axis_index("tensor")
    gain_row = gains[0]
    gate_matrix = w_gate[0, 0]
    up_matrix = w_up[0, 0]
    down_matrix = w_down[0, 0]

    def expert_work(arrived):
        gathered = gather_directly(arrived, "tensor", 0)
        row_count = gathered.shape[0] * gathered.shape[1]
        row_block = gathered.reshape(row_count, model_width)
        gate_val = jnp.dot(row_block, gate_matrix, preferred_element_type=jnp.float32)
        up_val = jnp.dot(row_block, up_matrix, preferred_element_type=jnp.float32)
        hidden = (jax.nn.silu(gate_val) * up_val).astype(jnp.bfloat16)
        partial_sum = jnp.dot(hidden, down_matrix, preferred_element_type=jnp.float32)
        summed = sum_at_owner(partial_sum.reshape(gathered.shape).astype(jnp.bfloat16), "tensor", 0)
        return summed.astype(jnp.bfloat16)

    def expert_layer(quarter_rows, chosen, micro_index):
        section_ids = route_ids[0, micro_index][chosen]
        section_weights = route_weights[0, micro_index][chosen]
        stream_f = quarter_rows.astype(jnp.float32)
        inv_rms = lax.rsqrt(jnp.mean(stream_f * stream_f, axis=1, keepdims=True) + epsilon)
        normed = (stream_f * inv_rms * gain_row[None, :]).astype(jnp.bfloat16)
        flat_ids = section_ids.reshape(-1)
        onehot = (flat_ids[:, None] == jnp.arange(groups, dtype=jnp.int32)[None, :]).astype(
            jnp.int32
        )
        earlier = jnp.cumsum(onehot, axis=0) - onehot
        slot_index = jnp.sum(earlier * onehot, axis=1)
        kept_mask = slot_index < capacity
        target = jnp.where(kept_mask, flat_ids * capacity + slot_index, groups * capacity)
        placing = (
            jnp.arange(groups * capacity, dtype=jnp.int32)[:, None] == target[None, :]
        ).astype(jnp.bfloat16)
        routed = jnp.repeat(normed, route_count, axis=0)
        outgoing = jnp.dot(placing, routed, preferred_element_type=jnp.float32).astype(jnp.bfloat16)
        outgoing = outgoing.reshape(groups, capacity, model_width)
        returned = expert_work(
            lax.all_to_all(outgoing, "expert", split_axis=0, concat_axis=0, tiled=True)
        )
        homeward = lax.all_to_all(returned, "expert", split_axis=0, concat_axis=0, tiled=True)
        flat_back = jnp.concatenate(
            [
                homeward.reshape(groups * capacity, model_width),
                jnp.zeros((1, model_width), jnp.bfloat16),
            ],
            axis=0,
        )
        picked = flat_back[target].astype(jnp.float32).reshape(quarter, route_count, model_width)
        kept_grid = kept_mask.reshape(quarter, route_count)
        weighted = picked * (section_weights * kept_grid)[..., None]
        update = jnp.sum(weighted, axis=1)
        return (stream_f + update).astype(jnp.bfloat16)

    def run_section(stream, micro_index):
        order_all = picks[0, micro_index, 0]
        chosen = lax.dynamic_slice_in_dim(order_all, my_rank * quarter, quarter)
        permuted = stream[order_all]
        quarter_rows = lax.all_to_all(permuted, "tensor", split_axis=0, concat_axis=1, tiled=True)
        fresh_rows = expert_layer(quarter_rows, chosen, micro_index)
        spread = lax.all_to_all(fresh_rows, "tensor", split_axis=1, concat_axis=0, tiled=True)
        return jnp.zeros_like(stream).at[order_all].set(spread)

    def first_input(micro_index):
        whole = tokens[micro_index]
        return lax.dynamic_slice_in_dim(whole, my_rank * slice_width, slice_width, 1)

    def send_on(fresh):
        return passed_along(fresh, "pipe", 1)

    def section_tick(carry, tick_index):
        arrived, collected = carry
        micro_index = tick_index - my_section
        active = (micro_index >= 0) & (micro_index < micro_count)
        clipped = jnp.clip(micro_index, 0, micro_count - 1)
        stream = jnp.where(my_section == 0, first_input(clipped), arrived)
        computed = run_section(stream, clipped)
        fresh = jnp.where(active, computed, stream)
        written = collected.at[clipped].set(fresh)
        collected = jnp.where(active, written, collected)
        return ((send_on(fresh), collected), None)

    empty_state = jnp.zeros((local_tokens, slice_width), jnp.bfloat16)
    collected = jnp.zeros((micro_count, local_tokens, slice_width), jnp.bfloat16)
    ticks = jnp.arange(micro_count + sections - 1, dtype=jnp.int32)
    (final_state, collected), unused = lax.scan(section_tick, (empty_state, collected), ticks)
    return collected[None]


def solution(mesh):
    return jax.shard_map(
        local,
        mesh=mesh,
        in_specs=(
            P(None, "expert", None),
            P("pipe", None),
            P("pipe", None, "expert", None),
            P("pipe", None, "expert", None),
            P("pipe", None, "expert", None),
            P("pipe", "expert", None, "tensor"),
            P("pipe", "expert", None, "tensor"),
            P("pipe", "expert", "tensor", None),
        ),
        out_specs=P("pipe", None, "expert", "tensor"),
        check_vma=False,
    )
```

profile of v0, /device:TPU:103, one launch (start us, length us, event | category | flops | bytes accessed | tf_op | source)
XLA Modules:
  0.0 1156.6 jit_solution(10860606724604831986)
XLA Ops:
  1.3 1155.4 %while.16 = (s32[]{:T(128)}, bf16[64,1024]{1,0:T(8,128)(2,1)S(1)}, bf16[2,64,1024]{2,1,0:T(8,128)(2,1)}, s32[9]{0:T(128)}, s32[]{:T(128)}, /*index=5*/s32[1,2,1,...) while((s32[]{:T(128)}, bf16[64,1024]{1,0:T(8,128)(2,1)S(1)}, ...), condition=%wide.region_8.9_spmd, body=%wide.region_0.8_spmd.sunk | while | flops 1523243264 | bytes 51076840 | solution.py:139
  16.2 23.3 %all_to_all.92 = bf16[8,5,4096]{2,1,0:T(8,128)(2,1)S(1)} all-to-all(bf16[8,5,4096]{2,1,0:T(8,128)(2,1)S(1)} %reshape.340), channel_id=1, replica_groups=mesh['pipe'=8,'tensor'=4,'expert'=8] {'expert'}, dimensions={0} | all-to-all | bytes 655360 | tf_op jit(solution)/shard_map/while/body/eval_jaxpr/all_to_all | solution.py:92
  39.9 18.8 %all_to_all.93 = bf16[4,8,5,4096]{3,1,2,0:T(8,128)(2,1)S(1)} all-to-all(bf16[4,8,5,4096]{3,1,2,0:T(8,128)(2,1)S(1)} %broadcast_in_dim.48), channel_id=1, replica_groups=mesh['pipe'=8,'tensor'=4,'expert'=8] {'tensor'}, dimensions={0} | all-to-all | bytes 2621440 | tf_op jit(solution)/shard_map/while/body/eval_jaxpr/all_to_all | solution.py:11
  145.1 22.9 %all_to_all.92 = bf16[8,5,4096]{2,1,0:T(8,128)(2,1)S(1)} all-to-all(bf16[8,5,4096]{2,1,0:T(8,128)(2,1)S(1)} %reshape.340), channel_id=1, replica_groups=mesh['pipe'=8,'tensor'=4,'expert'=8] {'expert'}, dimensions={0} | all-to-all | bytes 655360 | tf_op jit(solution)/shard_map/while/body/eval_jaxpr/all_to_all | solution.py:92
  168.4 19.4 %all_to_all.93 = bf16[4,8,5,4096]{3,1,2,0:T(8,128)(2,1)S(1)} all-to-all(bf16[4,8,5,4096]{3,1,2,0:T(8,128)(2,1)S(1)} %broadcast_in_dim.48), channel_id=1, replica_groups=mesh['pipe'=8,'tensor'=4,'expert'=8] {'tensor'}, dimensions={0} | all-to-all | bytes 2621440 | tf_op jit(solution)/shard_map/while/body/eval_jaxpr/all_to_all | solution.py:11
  273.4 22.7 %all_to_all.92 = bf16[8,5,4096]{2,1,0:T(8,128)(2,1)S(1)} all-to-all(bf16[8,5,4096]{2,1,0:T(8,128)(2,1)S(1)} %reshape.340), channel_id=1, replica_groups=mesh['pipe'=8,'tensor'=4,'expert'=8] {'expert'}, dimensions={0} | all-to-all | bytes 655360 | tf_op jit(solution)/shard_map/while/body/eval_jaxpr/all_to_all | solution.py:92
  296.6 19.4 %all_to_all.93 = bf16[4,8,5,4096]{3,1,2,0:T(8,128)(2,1)S(1)} all-to-all(bf16[4,8,5,4096]{3,1,2,0:T(8,128)(2,1)S(1)} %broadcast_in_dim.48), channel_id=1, replica_groups=mesh['pipe'=8,'tensor'=4,'expert'=8] {'tensor'}, dimensions={0} | all-to-all | bytes 2621440 | tf_op jit(solution)/shard_map/while/body/eval_jaxpr/all_to_all | solution.py:11
  401.6 22.7 %all_to_all.92 = bf16[8,5,4096]{2,1,0:T(8,128)(2,1)S(1)} all-to-all(bf16[8,5,4096]{2,1,0:T(8,128)(2,1)S(1)} %reshape.340), channel_id=1, replica_groups=mesh['pipe'=8,'tensor'=4,'expert'=8] {'expert'}, dimensions={0} | all-to-all | bytes 655360 | tf_op jit(solution)/shard_map/while/body/eval_jaxpr/all_to_all | solution.py:92
  424.7 19.4 %all_to_all.93 = bf16[4,8,5,4096]{3,1,2,0:T(8,128)(2,1)S(1)} all-to-all(bf16[4,8,5,4096]{3,1,2,0:T(8,128)(2,1)S(1)} %broadcast_in_dim.48), channel_id=1, replica_groups=mesh['pipe'=8,'tensor'=4,'expert'=8] {'tensor'}, dimensions={0} | all-to-all | bytes 2621440 | tf_op jit(solution)/shard_map/while/body/eval_jaxpr/all_to_all | solution.py:11
  459.0 16.0 %all-to-all-done.3 = bf16[4,8,5,4096]{3,1,2,0:T(8,128)(2,1)S(1)} async-done(((bf16[4,8,5,4096]{3,1,2,0:T(8,128)(2,1)}), bf16[4,8,5,4096]{3,1,2,0:T(8,128)(2,1)S(1)}, u32[]{:S(2)}, u32[]{:S(2)}) %all-to-all-start.3) | async-done | bytes 1310752 | tf_op jit(solution)/shard_map/while/body/eval_jaxpr/all_to_all | solution.py:32
  529.8 22.7 %all_to_all.92 = bf16[8,5,4096]{2,1,0:T(8,128)(2,1)S(1)} all-to-all(bf16[8,5,4096]{2,1,0:T(8,128)(2,1)S(1)} %reshape.340), channel_id=1, replica_groups=mesh['pipe'=8,'tensor'=4,'expert'=8] {'expert'}, dimensions={0} | all-to-all | bytes 655360 | tf_op jit(solution)/shard_map/while/body/eval_jaxpr/all_to_all | solution.py:92
  552.9 19.4 %all_to_all.93 = bf16[4,8,5,4096]{3,1,2,0:T(8,128)(2,1)S(1)} all-to-all(bf16[4,8,5,4096]{3,1,2,0:T(8,128)(2,1)S(1)} %broadcast_in_dim.48), channel_id=1, replica_groups=mesh['pipe'=8,'tensor'=4,'expert'=8] {'tensor'}, dimensions={0} | all-to-all | bytes 2621440 | tf_op jit(solution)/shard_map/while/body/eval_jaxpr/all_to_all | solution.py:11
  587.1 16.0 %all-to-all-done.3 = bf16[4,8,5,4096]{3,1,2,0:T(8,128)(2,1)S(1)} async-done(((bf16[4,8,5,4096]{3,1,2,0:T(8,128)(2,1)}), bf16[4,8,5,4096]{3,1,2,0:T(8,128)(2,1)S(1)}, u32[]{:S(2)}, u32[]{:S(2)}) %all-to-all-start.3) | async-done | bytes 1310752 | tf_op jit(solution)/shard_map/while/body/eval_jaxpr/all_to_all | solution.py:32
  658.0 22.7 %all_to_all.92 = bf16[8,5,4096]{2,1,0:T(8,128)(2,1)S(1)} all-to-all(bf16[8,5,4096]{2,1,0:T(8,128)(2,1)S(1)} %reshape.340), channel_id=1, replica_groups=mesh['pipe'=8,'tensor'=4,'expert'=8] {'expert'}, dimensions={0} | all-to-all | bytes 655360 | tf_op jit(solution)/shard_map/while/body/eval_jaxpr/all_to_all | solution.py:92
  681.0 19.4 %all_to_all.93 = bf16[4,8,5,4096]{3,1,2,0:T(8,128)(2,1)S(1)} all-to-all(bf16[4,8,5,4096]{3,1,2,0:T(8,128)(2,1)S(1)} %broadcast_in_dim.48), channel_id=1, replica_groups=mesh['pipe'=8,'tensor'=4,'expert'=8] {'tensor'}, dimensions={0} | all-to-all | bytes 2621440 | tf_op jit(solution)/shard_map/while/body/eval_jaxpr/all_to_all | solution.py:11
  715.3 16.0 %all-to-all-done.3 = bf16[4,8,5,4096]{3,1,2,0:T(8,128)(2,1)S(1)} async-done(((bf16[4,8,5,4096]{3,1,2,0:T(8,128)(2,1)}), bf16[4,8,5,4096]{3,1,2,0:T(8,128)(2,1)S(1)}, u32[]{:S(2)}, u32[]{:S(2)}) %all-to-all-start.3) | async-done | bytes 1310752 | tf_op jit(solution)/shard_map/while/body/eval_jaxpr/all_to_all | solution.py:32
  786.1 22.7 %all_to_all.92 = bf16[8,5,4096]{2,1,0:T(8,128)(2,1)S(1)} all-to-all(bf16[8,5,4096]{2,1,0:T(8,128)(2,1)S(1)} %reshape.340), channel_id=1, replica_groups=mesh['pipe'=8,'tensor'=4,'expert'=8] {'expert'}, dimensions={0} | all-to-all | bytes 655360 | tf_op jit(solution)/shard_map/while/body/eval_jaxpr/all_to_all | solution.py:92
  809.2 19.4 %all_to_all.93 = bf16[4,8,5,4096]{3,1,2,0:T(8,128)(2,1)S(1)} all-to-all(bf16[4,8,5,4096]{3,1,2,0:T(8,128)(2,1)S(1)} %broadcast_in_dim.48), channel_id=1, replica_groups=mesh['pipe'=8,'tensor'=4,'expert'=8] {'tensor'}, dimensions={0} | all-to-all | bytes 2621440 | tf_op jit(solution)/shard_map/while/body/eval_jaxpr/all_to_all | solution.py:11
  843.4 16.0 %all-to-all-done.3 = bf16[4,8,5,4096]{3,1,2,0:T(8,128)(2,1)S(1)} async-done(((bf16[4,8,5,4096]{3,1,2,0:T(8,128)(2,1)}), bf16[4,8,5,4096]{3,1,2,0:T(8,128)(2,1)S(1)}, u32[]{:S(2)}, u32[]{:S(2)}) %all-to-all-start.3) | async-done | bytes 1310752 | tf_op jit(solution)/shard_map/while/body/eval_jaxpr/all_to_all | solution.py:32
  914.3 22.7 %all_to_all.92 = bf16[8,5,4096]{2,1,0:T(8,128)(2,1)S(1)} all-to-all(bf16[8,5,4096]{2,1,0:T(8,128)(2,1)S(1)} %reshape.340), channel_id=1, replica_groups=mesh['pipe'=8,'tensor'=4,'expert'=8] {'expert'}, dimensions={0} | all-to-all | bytes 655360 | tf_op jit(solution)/shard_map/while/body/eval_jaxpr/all_to_all | solution.py:92
  937.4 19.4 %all_to_all.93 = bf16[4,8,5,4096]{3,1,2,0:T(8,128)(2,1)S(1)} all-to-all(bf16[4,8,5,4096]{3,1,2,0:T(8,128)(2,1)S(1)} %broadcast_in_dim.48), channel_id=1, replica_groups=mesh['pipe'=8,'tensor'=4,'expert'=8] {'tensor'}, dimensions={0} | all-to-all | bytes 2621440 | tf_op jit(solution)/shard_map/while/body/eval_jaxpr/all_to_all | solution.py:11
  971.6 16.0 %all-to-all-done.3 = bf16[4,8,5,4096]{3,1,2,0:T(8,128)(2,1)S(1)} async-done(((bf16[4,8,5,4096]{3,1,2,0:T(8,128)(2,1)}), bf16[4,8,5,4096]{3,1,2,0:T(8,128)(2,1)S(1)}, u32[]{:S(2)}, u32[]{:S(2)}) %all-to-all-start.3) | async-done | bytes 1310752 | tf_op jit(solution)/shard_map/while/body/eval_jaxpr/all_to_all | solution.py:32
  1042.4 22.7 %all_to_all.92 = bf16[8,5,4096]{2,1,0:T(8,128)(2,1)S(1)} all-to-all(bf16[8,5,4096]{2,1,0:T(8,128)(2,1)S(1)} %reshape.340), channel_id=1, replica_groups=mesh['pipe'=8,'tensor'=4,'expert'=8] {'expert'}, dimensions={0} | all-to-all | bytes 655360 | tf_op jit(solution)/shard_map/while/body/eval_jaxpr/all_to_all | solution.py:92
  1065.6 19.4 %all_to_all.93 = bf16[4,8,5,4096]{3,1,2,0:T(8,128)(2,1)S(1)} all-to-all(bf16[4,8,5,4096]{3,1,2,0:T(8,128)(2,1)S(1)} %broadcast_in_dim.48), channel_id=1, replica_groups=mesh['pipe'=8,'tensor'=4,'expert'=8] {'tensor'}, dimensions={0} | all-to-all | bytes 2621440 | tf_op jit(solution)/shard_map/while/body/eval_jaxpr/all_to_all | solution.py:11
  (727 shorter events, 688.8 us)
Async XLA Ops:
  6.1 9.0 all-to-all-start
  69.8 19.2 %all-to-all-start.3 = ((bf16[4,8,5,4096]{3,1,2,0:T(8,128)(2,1)}), bf16[4,8,5,4096]{3,1,2,0:T(8,128)(2,1)S(1)}, u32[]{:S(2)}, u32[]{:S(2)}) async-start(bf16[4,8,5,4096]{3,1,2,0:T(8,128)(2,1)} %copy.62), calls=%async_computation.3 | async-start | bytes 2621440 | tf_op jit(solution)/shard_map/while/body/eval_jaxpr/all_to_all | solution.py:32
  90.3 21.8 %all-to-all-start.4 = ((bf16[8,5,4096]{2,1,0:T(8,128)(2,1)}), bf16[8,5,4096]{2,1,0:T(8,128)(2,1)S(1)}, u32[]{:S(2)}, u32[]{:S(2)}) async-start(bf16[8,5,4096]{2,1,0:T(8,128)(2,1)} %copy.63), calls=%async_computation.4 | async-start | bytes 1048576 | tf_op jit(solution)/shard_map/while/body/eval_jaxpr/all_to_all | solution.py:94
  114.8 8.1 all-to-all-start.5
  136.0 8.1 all-to-all-start
  198.9 19.7 %all-to-all-start.3 = ((bf16[4,8,5,4096]{3,1,2,0:T(8,128)(2,1)}), bf16[4,8,5,4096]{3,1,2,0:T(8,128)(2,1)S(1)}, u32[]{:S(2)}, u32[]{:S(2)}) async-start(bf16[4,8,5,4096]{3,1,2,0:T(8,128)(2,1)} %copy.62), calls=%async_computation.3 | async-start | bytes 2621440 | tf_op jit(solution)/shard_map/while/body/eval_jaxpr/all_to_all | solution.py:32
  219.9 19.3 %all-to-all-start.4 = ((bf16[8,5,4096]{2,1,0:T(8,128)(2,1)}), bf16[8,5,4096]{2,1,0:T(8,128)(2,1)S(1)}, u32[]{:S(2)}, u32[]{:S(2)}) async-start(bf16[8,5,4096]{2,1,0:T(8,128)(2,1)} %copy.63), calls=%async_computation.4 | async-start | bytes 1048576 | tf_op jit(solution)/shard_map/while/body/eval_jaxpr/all_to_all | solution.py:94
  327.1 19.7 %all-to-all-start.3 = ((bf16[4,8,5,4096]{3,1,2,0:T(8,128)(2,1)}), bf16[4,8,5,4096]{3,1,2,0:T(8,128)(2,1)S(1)}, u32[]{:S(2)}, u32[]{:S(2)}) async-start(bf16[4,8,5,4096]{3,1,2,0:T(8,128)(2,1)} %copy.62), calls=%async_computation.3 | async-start | bytes 2621440 | tf_op jit(solution)/shard_map/while/body/eval_jaxpr/all_to_all | solution.py:32
  348.1 19.2 %all-to-all-start.4 = ((bf16[8,5,4096]{2,1,0:T(8,128)(2,1)}), bf16[8,5,4096]{2,1,0:T(8,128)(2,1)S(1)}, u32[]{:S(2)}, u32[]{:S(2)}) async-start(bf16[8,5,4096]{2,1,0:T(8,128)(2,1)} %copy.63), calls=%async_computation.4 | async-start | bytes 1048576 | tf_op jit(solution)/shard_map/while/body/eval_jaxpr/all_to_all | solution.py:94
  455.2 19.8 %all-to-all-start.3 = ((bf16[4,8,5,4096]{3,1,2,0:T(8,128)(2,1)}), bf16[4,8,5,4096]{3,1,2,0:T(8,128)(2,1)S(1)}, u32[]{:S(2)}, u32[]{:S(2)}) async-start(bf16[4,8,5,4096]{3,1,2,0:T(8,128)(2,1)} %copy.62), calls=%async_computation.3 | async-start | bytes 2621440 | tf_op jit(solution)/shard_map/while/body/eval_jaxpr/all_to_all | solution.py:32
  476.3 19.2 %all-to-all-start.4 = ((bf16[8,5,4096]{2,1,0:T(8,128)(2,1)}), bf16[8,5,4096]{2,1,0:T(8,128)(2,1)S(1)}, u32[]{:S(2)}, u32[]{:S(2)}) async-start(bf16[8,5,4096]{2,1,0:T(8,128)(2,1)} %copy.63), calls=%async_computation.4 | async-start | bytes 1048576 | tf_op jit(solution)/shard_map/while/body/eval_jaxpr/all_to_all | solution.py:94
  583.4 19.7 %all-to-all-start.3 = ((bf16[4,8,5,4096]{3,1,2,0:T(8,128)(2,1)}), bf16[4,8,5,4096]{3,1,2,0:T(8,128)(2,1)S(1)}, u32[]{:S(2)}, u32[]{:S(2)}) async-start(bf16[4,8,5,4096]{3,1,2,0:T(8,128)(2,1)} %copy.62), calls=%async_computation.3 | async-start | bytes 2621440 | tf_op jit(solution)/shard_map/while/body/eval_jaxpr/all_to_all | solution.py:32
  604.4 19.2 %all-to-all-start.4 = ((bf16[8,5,4096]{2,1,0:T(8,128)(2,1)}), bf16[8,5,4096]{2,1,0:T(8,128)(2,1)S(1)}, u32[]{:S(2)}, u32[]{:S(2)}) async-start(bf16[8,5,4096]{2,1,0:T(8,128)(2,1)} %copy.63), calls=%async_computation.4 | async-start | bytes 1048576 | tf_op jit(solution)/shard_map/while/body/eval_jaxpr/all_to_all | solution.py:94
  626.4 8.1 all-to-all-start.5
  711.6 19.8 %all-to-all-start.3 = ((bf16[4,8,5,4096]{3,1,2,0:T(8,128)(2,1)}), bf16[4,8,5,4096]{3,1,2,0:T(8,128)(2,1)S(1)}, u32[]{:S(2)}, u32[]{:S(2)}) async-start(bf16[4,8,5,4096]{3,1,2,0:T(8,128)(2,1)} %copy.62), calls=%async_computation.3 | async-start | bytes 2621440 | tf_op jit(solution)/shard_map/while/body/eval_jaxpr/all_to_all | solution.py:32
  732.6 19.2 %all-to-all-start.4 = ((bf16[8,5,4096]{2,1,0:T(8,128)(2,1)}), bf16[8,5,4096]{2,1,0:T(8,128)(2,1)S(1)}, u32[]{:S(2)}, u32[]{:S(2)}) async-start(bf16[8,5,4096]{2,1,0:T(8,128)(2,1)} %copy.63), calls=%async_computation.4 | async-start | bytes 1048576 | tf_op jit(solution)/shard_map/while/body/eval_jaxpr/all_to_all | solution.py:94
  754.5 8.1 all-to-all-start.5
  839.7 19.8 %all-to-all-start.3 = ((bf16[4,8,5,4096]{3,1,2,0:T(8,128)(2,1)}), bf16[4,8,5,4096]{3,1,2,0:T(8,128)(2,1)S(1)}, u32[]{:S(2)}, u32[]{:S(2)}) async-start(bf16[4,8,5,4096]{3,1,2,0:T(8,128)(2,1)} %copy.62), calls=%async_computation.3 | async-start | bytes 2621440 | tf_op jit(solution)/shard_map/while/body/eval_jaxpr/all_to_all | solution.py:32
  860.7 19.2 %all-to-all-start.4 = ((bf16[8,5,4096]{2,1,0:T(8,128)(2,1)}), bf16[8,5,4096]{2,1,0:T(8,128)(2,1)S(1)}, u32[]{:S(2)}, u32[]{:S(2)}) async-start(bf16[8,5,4096]{2,1,0:T(8,128)(2,1)} %copy.63), calls=%async_computation.4 | async-start | bytes 1048576 | tf_op jit(solution)/shard_map/while/body/eval_jaxpr/all_to_all | solution.py:94
  967.9 19.8 %all-to-all-start.3 = ((bf16[4,8,5,4096]{3,1,2,0:T(8,128)(2,1)}), bf16[4,8,5,4096]{3,1,2,0:T(8,128)(2,1)S(1)}, u32[]{:S(2)}, u32[]{:S(2)}) async-start(bf16[4,8,5,4096]{3,1,2,0:T(8,128)(2,1)} %copy.62), calls=%async_computation.3 | async-start | bytes 2621440 | tf_op jit(solution)/shard_map/while/body/eval_jaxpr/all_to_all | solution.py:32
  988.9 19.2 %all-to-all-start.4 = ((bf16[8,5,4096]{2,1,0:T(8,128)(2,1)}), bf16[8,5,4096]{2,1,0:T(8,128)(2,1)S(1)}, u32[]{:S(2)}, u32[]{:S(2)}) async-start(bf16[8,5,4096]{2,1,0:T(8,128)(2,1)} %copy.63), calls=%async_computation.4 | async-start | bytes 1048576 | tf_op jit(solution)/shard_map/while/body/eval_jaxpr/all_to_all | solution.py:94
  1096.1 19.7 %all-to-all-start.3 = ((bf16[4,8,5,4096]{3,1,2,0:T(8,128)(2,1)}), bf16[4,8,5,4096]{3,1,2,0:T(8,128)(2,1)S(1)}, u32[]{:S(2)}, u32[]{:S(2)}) async-start(bf16[4,8,5,4096]{3,1,2,0:T(8,128)(2,1)} %copy.62), calls=%async_computation.3 | async-start | bytes 2621440 | tf_op jit(solution)/shard_map/while/body/eval_jaxpr/all_to_all | solution.py:32
  1117.1 19.2 %all-to-all-start.4 = ((bf16[8,5,4096]{2,1,0:T(8,128)(2,1)}), bf16[8,5,4096]{2,1,0:T(8,128)(2,1)S(1)}, u32[]{:S(2)}, u32[]{:S(2)}) async-start(bf16[8,5,4096]{2,1,0:T(8,128)(2,1)} %copy.63), calls=%async_computation.4 | async-start | bytes 1048576 | tf_op jit(solution)/shard_map/while/body/eval_jaxpr/all_to_all | solution.py:94
  1139.0 8.1 all-to-all-start.5
  (102 other events, 1014.4 us)
where the time goes:
time: 1180 us; the launch traced here: 1160 us
  blocking collectives  379 us (32%)
  waiting for transfers between devices  365 us (31%)
  starting transfers between devices  166 us (14%)
  local copies, waits for them, and re-layouts  115 us (10%)
  matrix products  67.2 us (6%)
  other arithmetic  56.2 us (5%)
    all_to_all x9, blocking collectives, expert_layer(): lax.all_to_all(outgoing, 'expert', split_axis=0, concat_axis=0, tiled=True)  205 us
    all_to_all x9, blocking collectives, from_everyone(): return lax.all_to_all(copies, axis, split_axis=0, concat_axis=0, tiled=True)  174 us
    all_to_all x9, waiting for transfers between devices, sum_at_owner(): lax.all_to_all(pieces, axis, split_axis=0, concat_axis=0, tiled=True)  144 us
    all_to_all x9, waiting for transfers between devices, expert_layer(): lax.all_to_all(returned, 'expert', split_axis=0, concat_axis=0, tiled=True)  107 us
    all_to_all x9, starting transfers between devices, expert_layer(): lax.all_to_all(returned, 'expert', split_axis=0, concat_axis=0, tiled=True)  60.7 us
    ppermute x9, waiting for transfers between devices, passed_along(): return lax.ppermute(block, axis, route)  57.4 us
    dot_general x9, matrix products, expert_work(): jnp.dot(hidden, down_matrix, preferred_element_type=jnp.float32)  40.5 us
    all_to_all x9, waiting for transfers between devices, run_section(): lax.all_to_all(fresh_rows, 'tensor', split_axis=1, concat_axis=0, tiled=T...  36 us
  transfers between devices with their start and end apart: 45, of which 45 were waited for; matrix products, arithmetic and copies ran while one was open for 3% of the time, Pallas kernels for 0%

commit v1 on v0

v1 whole, which is shorter than its diff:
```python
import functools

import jax
import jax.numpy as jnp
import numpy as np
from jax import lax
from jax.experimental import pallas as pl
from jax.experimental.pallas import tpu as pltpu
from jax.sharding import PartitionSpec as P

EPS = 1e-06
CAP = 5
ROWS = 16
BLOCKS = 4
F32 = jnp.float32
BF16 = jnp.bfloat16
MESH = pl.DeviceIdType.MESH


def dot(a, b):
    return jnp.dot(a, b, preferred_element_type=F32)


def kernel(
    sizes,
    tok_hbm,
    wg_hbm,
    wu_hbm,
    wd_hbm,
    gain_ref,
    pm_ref,
    pe_ref,
    cm_ref,
    ce_ref,
    pi_ref,
    pit_ref,
    out_ref,
    w1,
    w2,
    x_buf,
    xs,
    acc,
    part_out,
    part_in,
    first_msg,
    next_msg,
    back_out,
    back_in,
    h_buf,
    w_sem,
    tok_sem,
    a1_send,
    a1_recv,
    a2_send,
    a2_recv,
    b1_send,
    b1_recv,
    b2_send,
    b2_recv,
    h_send,
    h_recv,
):
    stages, ranks, experts, micro, group = sizes
    sets = experts // group
    chunks = micro * sets
    width = h_buf.shape[2]
    narrow = width // BLOCKS
    hidden = w2.shape[1]
    main_rows = group * ROWS
    extra_rows = xs.shape[1] - main_rows
    model = width * ranks
    tok = h_buf.shape[1]
    p = lax.axis_index("pipe")
    t = lax.axis_index("tensor")
    me = lax.axis_index("expert")
    my_set = lax.rem(me, sets)
    my_place = me // sets

    def peer(i):
        return lax.rem(t + i, ranks)

    def other(i):
        return lax.rem(me + i, experts)

    def remote(src, dst, send, recv, where):
        return pltpu.make_async_remote_copy(
            src_ref=src, dst_ref=dst, send_sem=send, recv_sem=recv, device_id=where, device_id_type=MESH
        )

    loads = []
    for f in range(ranks):
        rows = pl.ds(f * width, width)
        loads.append(pltpu.make_async_copy(wg_hbm.at[rows, :], w1.at[f, :, pl.ds(0, hidden)], w_sem.at[f]))
        loads.append(pltpu.make_async_copy(wu_hbm.at[rows, :], w1.at[f, :, pl.ds(hidden, hidden)], w_sem.at[ranks + f]))
        loads.append(pltpu.make_async_copy(wd_hbm.at[:, rows], w2.at[f], w_sem.at[2 * ranks + f]))
    slice_start = pl.multiple_of(t * width, 128)
    tok_load = pltpu.make_async_copy(tok_hbm.at[:, :, pl.ds(slice_start, width)], h_buf, tok_sem)

    @pl.when(p == 0)
    def _():
        tok_load.start()

    for load in loads:
        load.start()

    barrier = pltpu.get_barrier_semaphore()
    for i in range(1, ranks):
        pl.semaphore_signal(barrier, inc=1, device_id={"tensor": peer(i)}, device_id_type=MESH)
    for i in range(1, experts):
        pl.semaphore_signal(barrier, inc=1, device_id={"expert": other(i)}, device_id_type=MESH)

    @pl.when(p < stages - 1)
    def _():
        for e in range(experts):
            pl.semaphore_signal(barrier, inc=1, device_id={"pipe": p + 1, "expert": e}, device_id_type=MESH)

    @pl.when(p > 0)
    def _():
        for e in range(experts):
            pl.semaphore_signal(barrier, inc=1, device_id={"pipe": p - 1, "expert": e}, device_id_type=MESH)

    ahead = jnp.where(p < stages - 1, experts, 0)
    behind = jnp.where(p > 0, experts, 0)
    pl.semaphore_wait(barrier, ranks - 1 + experts - 1 + ahead + behind)

    def fill_messages(msg, which, m, stream):
        main = dot(pm_ref[which, m], stream).astype(BF16)
        stacked = jnp.concatenate([stream[:, b * narrow : (b + 1) * narrow] for b in range(BLOCKS)], axis=0)
        extra = dot(pe_ref[which, m], stacked).astype(BF16)
        for e in range(experts):
            msg[m, e, :, pl.ds(0, width)] = main[e * ROWS : (e + 1) * ROWS]
            msg[m, e, :, pl.ds(width, narrow)] = extra[e * ROWS : (e + 1) * ROWS]

    def first_copy(m, i):
        e = other(i)
        c = m * sets + my_set
        return remote(
            first_msg.at[m, e],
            x_buf.at[c, t, my_place],
            a1_send.at[0, m, e],
            a1_recv.at[c, my_place],
            {"expert": e},
        )

    def next_copy(m, e):
        c = m * sets + my_set
        return remote(
            next_msg.at[m, e],
            x_buf.at[c, t, my_place],
            a1_send.at[1, m, e],
            a1_recv.at[c, my_place],
            {"pipe": p + 1, "expert": e},
        )

    def stream_copy(m):
        return remote(out_ref.at[m], h_buf.at[m], h_send.at[m], h_recv.at[m], {"pipe": p + 1})

    def relay_copy(c, j, i):
        return remote(
            x_buf.at[c, t, j], x_buf.at[c, t, j], a2_send.at[c, j, i - 1], a2_recv.at[c, t, j], {"tensor": peer(i)}
        )

    def part_copy(c, i):
        return remote(
            part_out.at[c, i - 1], part_in.at[c, t], b1_send.at[c, i - 1], b1_recv.at[c, t], {"tensor": peer(i)}
        )

    def back_copy(c, j):
        m = c // sets
        g = j * sets + lax.rem(c, sets)
        return remote(back_out.at[c, j], back_in.at[m, me], b2_send.at[c, j], b2_recv.at[m, me], {"expert": g})

    @pl.when(p == 0)
    def _():
        tok_load.wait()
        for m in range(micro):
            fill_messages(first_msg, 0, m, h_buf[m])
            for i in range(1, experts):
                first_copy(m, i).start()
            x_buf[m * sets + my_set, t, my_place] = first_msg[m, me]

    for load in loads:
        load.wait()

    def relay(c):
        for j in range(group):
            g = j * sets + lax.rem(c, sets)

            @pl.when((p > 0) | (g != me))
            def _():
                remote(
                    first_msg.at[0, 0], x_buf.at[c, t, j], a1_send.at[0, 0, 0], a1_recv.at[c, j], {"expert": other(1)}
                ).wait_recv()

            for i in (2, 1, 3):
                relay_copy(c, j, i).start()

    def experts_work(c):
        total = None
        squares = None
        for i in (0, 1, 3, 2):
            f = peer(i)
            if i > 0:
                for j in range(group):
                    remote(
                        x_buf.at[c, f, j], x_buf.at[c, f, j], a2_send.at[c, j, i - 1], a2_recv.at[c, f, j], {"tensor": f}
                    ).wait_recv()
            gain = gain_ref[f]
            main = x_buf[c, f, :, :, pl.ds(0, width)].reshape(main_rows, width).astype(F32)
            xs[f, pl.ds(0, main_rows), :] = (main * gain).astype(BF16)
            packed = x_buf[c, f, :, :, pl.ds(width, narrow)].reshape(main_rows, narrow)
            extra = dot(pi_ref[...], packed)
            extra_sq = jnp.zeros((extra_rows, 1), F32)
            for b in range(BLOCKS):
                block = extra[b * extra_rows : (b + 1) * extra_rows]
                cols = slice(b * narrow, (b + 1) * narrow)
                extra_sq = extra_sq + jnp.sum(block * block, axis=1, keepdims=True)
                xs[f, pl.ds(main_rows, extra_rows), pl.ds(b * narrow, narrow)] = (block * gain[:, cols]).astype(BF16)
            sq = jnp.concatenate([jnp.sum(main * main, axis=1, keepdims=True), extra_sq], axis=0)
            squares = sq if squares is None else squares + sq
            if i == 0:
                acc[...] = dot(xs[f], w1[f])
            else:
                acc[...] += dot(xs[f], w1[f])
        inv = lax.rsqrt(squares * (1.0 / model) + EPS)
        gate = acc[:, pl.ds(0, hidden)] * inv
        up = acc[:, pl.ds(hidden, hidden)] * inv
        act = (gate / (1.0 + jnp.exp(-gate)) * up).astype(BF16)
        for i in (2, 1, 3, 0):
            part = dot(act, w2[peer(i)]).astype(BF16)
            if i == 0:
                part_in[c, t] = part
            else:
                part_out[c, i - 1] = part
                part_copy(c, i).start()

    def give_back(c):
        m = c // sets
        for i in range(1, ranks):
            f = peer(i)
            remote(part_out.at[c, i - 1], part_in.at[c, f], b1_send.at[c, i - 1], b1_recv.at[c, f], {"tensor": f}).wait_recv()
        total = part_in[c, 0].astype(F32)
        for q in range(1, ranks):
            total = total + part_in[c, q].astype(F32)
        total = total.astype(BF16)
        extra = total[main_rows:]
        stacked = jnp.concatenate([extra[:, b * narrow : (b + 1) * narrow] for b in range(BLOCKS)], axis=0)
        packed = dot(pit_ref[...], stacked).astype(BF16)
        for j in range(group):
            back_out[c, j, :, pl.ds(0, width)] = total[j * ROWS : (j + 1) * ROWS]
            back_out[c, j, :, pl.ds(width, narrow)] = packed[j * ROWS : (j + 1) * ROWS]
        for j in range(group):
            g = j * sets + lax.rem(c, sets)

            @pl.when(g != me)
            def _():
                back_copy(c, j).start()

            @pl.when(g == me)
            def _():
                back_in[m, me] = back_out[c, j]

    def combine(c):
        m = c // sets

        @pl.when(lax.rem(c, sets) == my_set)
        def _():
            for i in range(1, experts):
                e = other(i)
                remote(back_out.at[c, 0], back_in.at[m, e], b2_send.at[c, 0], b2_recv.at[m, e], {"expert": e}).wait_recv()

            @pl.when(p > 0)
            def _():
                remote(out_ref.at[m], h_buf.at[m], h_send.at[m], h_recv.at[m], {"expert": other(1)}).wait_recv()

            main = back_in[m, :, :, pl.ds(0, width)].reshape(experts * ROWS, width)
            packed = back_in[m, :, :, pl.ds(width, narrow)].reshape(experts * ROWS, narrow)
            wide = dot(cm_ref[m], main)
            update = wide[:tok] + wide[tok:]
            thin = dot(ce_ref[m], packed)
            thin = thin[: BLOCKS * tok] + thin[BLOCKS * tok :]
            spread = jnp.concatenate([thin[b * tok : (b + 1) * tok] for b in range(BLOCKS)], axis=1)
            fresh = (h_buf[m].astype(F32) + update + spread).astype(BF16)
            out_ref[m] = fresh

            @pl.when(p < stages - 1)
            def _():
                fill_messages(next_msg, 1, m, fresh)
                for e in range(experts):
                    next_copy(m, e).start()
                stream_copy(m).start()

    def step(s, carry):
        @pl.when(s < chunks)
        def _():
            relay(s)

        @pl.when(s > 0)
        def _():
            give_back(s - 1)

        @pl.when(s < chunks)
        def _():
            experts_work(s)

        @pl.when(s > 0)
        def _():
            combine(s - 1)

        return carry

    lax.fori_loop(0, chunks + 1, step, 0)

    @pl.when(p == 0)
    def _():
        for m in range(micro):
            for i in range(1, experts):
                first_copy(m, i).wait_send()

    @pl.when(p < stages - 1)
    def _():
        for m in range(micro):
            for e in range(experts):
                next_copy(m, e).wait_send()
            stream_copy(m).wait_send()

    def drain(c, carry):
        for j in range(group):
            for i in range(1, ranks):
                relay_copy(c, j, i).wait_send()
            g = j * sets + lax.rem(c, sets)

            @pl.when(g != me)
            def _():
                back_copy(c, j).wait_send()

        for i in range(1, ranks):
            part_copy(c, i).wait_send()
        return carry

    lax.fori_loop(0, chunks, drain, 0)


def positions(ids, weights, order, experts, ranks):
    tok = order.shape[-1]
    index = jnp.arange(tok, dtype=jnp.int32)
    rank = jnp.sum(jnp.where(order[:, :, None] == index[None, None, :], index[None, :, None], 0), axis=1)
    quarter = rank // (tok // ranks)
    names = ids[..., None] == jnp.arange(experts, dtype=jnp.int32)
    named = jnp.any(names, axis=2)
    weight = jnp.sum(jnp.where(names, weights[..., None], 0.0), axis=2)
    before = (quarter[:, :, None] == quarter[:, None, :]) & (rank[:, None, :] < rank[:, :, None])
    slot = jnp.sum((before[..., None] & named[:, None]).astype(jnp.int32), axis=2)
    kept = named & (slot < CAP)
    return jnp.where(kept, quarter[..., None] * CAP + slot, -1), weight


def placing(pos):
    micro, tok, experts = pos.shape
    by_expert = jnp.swapaxes(pos, 1, 2)[:, :, None, :]
    main = by_expert == jnp.arange(ROWS, dtype=jnp.int32)[None, None, :, None]
    k = jnp.arange(BLOCKS, dtype=jnp.int32)
    extra = by_expert[:, :, None, :, None, :] == (ROWS + k)[None, None, None, :, None, None]
    same = k[:, None] == k[None, :]
    extra = extra & same[None, None, :, None, :, None]
    main = main.reshape(micro, experts * ROWS, tok).astype(BF16)
    extra = extra.reshape(micro, experts * ROWS, BLOCKS * tok).astype(BF16)
    return main, extra


def gathering(pos, weight):
    micro, tok, experts = pos.shape
    high = weight.astype(BF16).astype(F32)
    both = jnp.stack([high, weight - high], axis=1)[..., None]
    main = jnp.where((pos[..., None] == jnp.arange(ROWS, dtype=jnp.int32))[:, None], both, 0.0)
    k = jnp.arange(BLOCKS, dtype=jnp.int32)
    extra = jnp.where((pos[..., None] == ROWS + k)[:, None], both, 0.0)
    same = k[:, None] == k[None, :]
    extra = jnp.where(same[None, None, :, None, None, :, None], extra[:, :, None, :, :, None, :], 0.0)
    main = main.reshape(micro, 2 * tok, experts * ROWS).astype(BF16)
    extra = extra.reshape(micro, 2 * BLOCKS * tok, experts * ROWS).astype(BF16)
    return main, extra


def local(sizes, tokens, gains, route_ids, route_weights, picks, w_gate, w_up, w_down):
    stages, ranks, experts, micro, group = sizes
    tok, model = tokens.shape[1:]
    width = model // ranks
    narrow = width // BLOCKS
    wide = width + narrow
    hidden = w_gate.shape[3]
    chunks = micro * (experts // group)
    main_rows = group * ROWS
    extra_rows = max(ROWS, BLOCKS * group)
    rows = main_rows + extra_rows

    pos, weight = positions(route_ids[0], route_weights[0], picks[0, :, 0], experts, ranks)
    following = lax.ppermute(pos, "pipe", [(i + 1, i) for i in range(stages - 1)])
    pm, pe = placing(jnp.concatenate([pos, following], axis=0))
    pm = pm.reshape(2, micro, *pm.shape[1:])
    pe = pe.reshape(2, micro, *pe.shape[1:])
    cm, ce = gathering(pos, weight)

    permute = np.zeros((BLOCKS, extra_rows, group, BLOCKS, BLOCKS), np.float32)
    for b in range(BLOCKS):
        for j in range(group):
            for k in range(BLOCKS):
                permute[b, j * BLOCKS + k, j, b, k] = 1.0
    permute = permute.reshape(BLOCKS * extra_rows, main_rows)
    pi = jnp.asarray(permute, BF16)
    pit = jnp.asarray(permute.T.copy(), BF16)

    vmem = pl.BlockSpec(memory_space=pltpu.VMEM)
    hbm = pl.BlockSpec(memory_space=pl.ANY)
    dma = pltpu.SemaphoreType.DMA
    out = pl.pallas_call(
        functools.partial(kernel, sizes),
        out_shape=jax.ShapeDtypeStruct((micro, tok, width), BF16),
        in_specs=[hbm] * 4 + [vmem] * 7,
        out_specs=vmem,
        scratch_shapes=[
            pltpu.VMEM((ranks, width, 2 * hidden), BF16),
            pltpu.VMEM((ranks, hidden, width), BF16),
            pltpu.VMEM((chunks, ranks, group, ROWS, wide), BF16),
            pltpu.VMEM((ranks, rows, width), BF16),
            pltpu.VMEM((rows, 2 * hidden), F32),
            pltpu.VMEM((chunks, ranks - 1, rows, width), BF16),
            pltpu.VMEM((chunks, ranks, rows, width), BF16),
            pltpu.VMEM((micro, experts, ROWS, wide), BF16),
            pltpu.VMEM((micro, experts, ROWS, wide), BF16),
            pltpu.VMEM((chunks, group, ROWS, wide), BF16),
            pltpu.VMEM((micro, experts, ROWS, wide), BF16),
            pltpu.VMEM((micro, tok, width), BF16),
            dma((3 * ranks,)),
            dma,
            dma((2, micro, experts)),
            dma((chunks, group)),
            dma((chunks, group, ranks - 1)),
            dma((chunks, ranks, group)),
            dma((chunks, ranks - 1)),
            dma((chunks, ranks)),
            dma((chunks, group)),
            dma((micro, experts)),
            dma((micro,)),
            dma((micro,)),
        ],
        compiler_params=pltpu.CompilerParams(
            collective_id=0, has_side_effects=True, vmem_limit_bytes=60_000_000
        ),
    )(
        tokens,
        w_gate[0, 0],
        w_up[0, 0],
        w_down[0, 0],
        gains.reshape(ranks, 1, width),
        pm,
        pe,
        cm,
        ce,
        pi,
        pit,
    )
    return out[None]


def solution(mesh, group=2):
    experts = mesh.shape["expert"]
    sizes = (mesh.shape["pipe"], mesh.shape["tensor"], experts, 2, min(group, experts))
    return jax.shard_map(
        functools.partial(local, sizes),
        mesh=mesh,
        in_specs=(
            P(None, "expert", None),
            P("pipe", None),
            P("pipe", None, "expert", None),
            P("pipe", None, "expert", None),
            P("pipe", None, "expert", None),
            P("pipe", "expert", None, "tensor"),
            P("pipe", "expert", None, "tensor"),
            P("pipe", "expert", "tensor", None),
        ),
        out_specs=P("pipe", None, "expert", "tensor"),
        check_vma=False,
    )
```

time: 1180 us -> 316 us (0.27); the launches traced: 1160 us -> 316 us
  blocking collectives: 379 us -> 0 us
  waiting for transfers between devices: 365 us -> 0.01 us
  Pallas kernels: 0 us -> 302 us
  starting transfers between devices: 166 us -> 1.73 us
  local copies, waits for them, and re-layouts: 115 us -> 4.82 us
  matrix products: 67.2 us -> 0 us
  other arithmetic: 56.2 us -> 7.26 us
    all_to_all x18 -> x0, blocking collectives: 379 us -> none  [the longest x9 205 us: expert_layer(): lax.all_to_all(outgoing, 'expert', split_axis=0, concat_axis=0, tiled=True)]
    all_to_all x36 -> x0, waiting for transfers between devices: 307 us -> none  [the longest x9 144 us: sum_at_owner(): lax.all_to_all(pieces, axis, split_axis=0, concat_axis=0, tiled=True)]
    pallas_call x0 -> x1, Pallas kernels: none -> 302 us  [local(): pl.pallas_call(functools.partial(kernel, sizes), out_shape=jax.ShapeDtype...]
    all_to_all x36 -> x0, starting transfers between devices: 154 us -> none  [the longest x9 60.7 us: expert_layer(): lax.all_to_all(returned, 'expert', split_axis=0, concat_axis=0, tiled=True)]
    dot_general x27 -> x0, matrix products: 67.2 us -> none  [the longest x9 40.5 us: expert_work(): jnp.dot(hidden, down_matrix, preferred_element_type=jnp.float32)]
    ppermute x9 -> x1, waiting for transfers between devices: 57.4 us -> 0.01 us  [local(): lax.ppermute(pos, 'pipe', [(i + 1, i) for i in range(stages - 1)])]
    gather x36 -> x0, local copies, waits for them, and re-layouts: 28.7 us -> none  [the longest x9 12.2 us: run_section(): permuted = stream[order_all]]
    select_n x54 -> x2, other arithmetic: 28.5 us -> 0.06 us  [the longest x1 0.05 us: gathering(): extra = jnp.where((pos[..., None] == ROWS + k)[:, None], both, 0.0)]
  transfers between devices with their start and end apart: 45 -> 1, of which waited for: 45 -> 0; matrix products, arithmetic and copies ran while one was open for 3% -> 1% of each run, Pallas kernels for 0% -> 0%
where the time goes in v1:
time: 316 us
  Pallas kernels  302 us (96%)
  other arithmetic  7.26 us (2%)
  local copies, waits for them, and re-layouts  4.82 us (2%)
    pallas_call x1, Pallas kernels, local(): pl.pallas_call(functools.partial(kernel, sizes), out_shape=jax.ShapeDtype...  302 us
  transfers between devices with their start and end apart: 1, of which 0 were waited for; matrix products, arithmetic and copies ran while one was open for 1% of the time, Pallas kernels for 0%

profile of v1, /device:TPU:103, one launch (start us, length us, event | category | flops | bytes accessed | tf_op | source)
XLA Modules:
  0.0 315.6 jit_solution(14272299669222355842)
XLA Ops:
  0.0 0.8 select_reduce_fusion
  0.9 0.7 fusion
  1.6 2.2 convert_reduce_fusion
  3.9 1.7 collective-permute-start
  5.7 0.7 select_reduce_fusion.1
  6.6 0.1 broadcast_in_dim.141
  6.8 0.3 broadcast_in_dim.142
  7.1 0.2 copy.29
  7.3 0.1 broadcast_in_dim.135
  7.4 0.2 broadcast_in_dim.136
  7.6 0.2 copy.27
  7.8 0.8 select_convert_fusion.ce_ref
  8.6 0.2 select_convert_fusion.1
  8.7 0.1 copy.25
  8.8 0.1 and.83
  9.0 0.2 and.84
  9.2 0.1 convert_element_type.53
  9.3 0.7 copy.30.cm_ref
  10.2 0.1 and.81
  10.3 0.5 and.82
  10.8 0.8 and_convert_fusion.pe_ref
  11.6 0.7 compare_convert_fusion.pm_ref
  12.3 301.6 %shard_map.100 = bf16[2,64,1024]{2,1,0:T(8,128)(2,1)} custom-call(bf16[2,64,4096]{2,1,0:T(8,128)(2,1)} %tok_hbm.1, bf16[4096,384]{1,0:T(8,128)(2,1)} %bitcast.24, bf16[4096,384]{1,0:T(8,128)(2,1)} %bitcast.25, bf16[384,4096]{1,0:T(8,128)(2,1)} %bitcast.26, f32[4,1,1024]{2,1,0:T(1,128)} %bitcast.29, bf16[2,2,128,64]{3,2,1,0:T(8,128)(2,1)} %compare_convert_fusion.pm_ref, ...), custom_call_target="tpu_custom_call" | custom-call | tf_op jit(solution)/shard_map/pallas_call | solution.py:416
  313.9 1.7 copy.32
  (19 shorter events, 0.6 us)
Async XLA Ops:
  3.9 6.2 %collective-permute-start = (s32[2,64,8]{1,2,0:T(8,128)S(1)}, s32[2,64,8]{1,2,0:T(8,128)S(1)}, u32[]{:S(2)}, u32[]{:S(2)}) collective-permute-start(s32[2,64,8]{1,2,0:T(8,128)S(1)} %add_select_fusion), channel_id=1, source_target_pairs={{32,0},{64,32},{96,64},{128,96},{160,128},{192,160},{224,192},{33,... | collective-permute-start | bytes 12296 | tf_op jit(solution)/shard_map/ppermute | solution.py:398

commit v2 on v1

--- a/solution.py
+++ b/solution.py
@@ -28,13 +28,20 @@
     wu_hbm,
     wd_hbm,
     gain_ref,
+    ids_ref,
+    idst_ref,
+    wt_ref,
+    row_ref,
+    col_ref,
+    pi_ref,
+    pit_ref,
+    out_ref,
     pm_ref,
     pe_ref,
     cm_ref,
     ce_ref,
-    pi_ref,
-    pit_ref,
-    out_ref,
+    post,
+    pos_tok,
     w1,
     w2,
     x_buf,
@@ -59,6 +66,8 @@
     b2_recv,
     h_send,
     h_recv,
+    post_send,
+    post_recv,
 ):
     stages, ranks, experts, micro, group = sizes
     sets = experts // group
@@ -82,6 +91,11 @@
     def other(i):
         return lax.rem(me + i, experts)
 
+    order = sorted(range(experts), key=lambda i: -min(i // 2, (experts - 1 - i) // 2 + 1 if i > 1 else 0))
+
+    def other_chip(i):
+        return lax.rem(me - lax.rem(me, 2) + i, experts)
+
     def remote(src, dst, send, recv, where):
         return pltpu.make_async_remote_copy(
             src_ref=src, dst_ref=dst, send_sem=send, recv_sem=recv, device_id=where, device_id_type=MESH
@@ -102,6 +116,65 @@
 
     for load in loads:
         load.start()
+
+    def count(shape, dim):
+        return lax.broadcasted_iota(jnp.int32, shape, dim)
+
+    def slots(m):
+        across, down = count((tok, tok), 1), count((tok, tok), 0)
+        rank_row = jnp.sum(jnp.where(col_ref[m] == across, down.astype(F32), 0.0), axis=0, keepdims=True)
+        rank_col = jnp.sum(jnp.where(row_ref[m] == down, across.astype(F32), 0.0), axis=1, keepdims=True)
+        part_row = jnp.floor(rank_row * (ranks / tok))
+        part_col = jnp.floor(rank_col * (ranks / tok))
+        same = jnp.where(part_row == part_col, 1.0, 0.0)
+        before_t = (jnp.where(rank_col < rank_row, 1.0, 0.0) * same).astype(BF16)
+        before = (jnp.where(rank_row < rank_col, 1.0, 0.0) * same).astype(BF16)
+        e_down, e_across = count((experts, tok), 0), count((tok, experts), 1)
+        ids, idst = ids_ref[m], idst_ref[m]
+        named_t = jnp.where((idst[0:1] == e_down) | (idst[1:2] == e_down), 1.0, 0.0)
+        named = jnp.where((ids[:, 0:1] == e_across) | (ids[:, 1:2] == e_across), 1.0, 0.0)
+        slot_t = dot(named_t.astype(BF16), before_t)
+        slot = dot(before, named.astype(BF16))
+        post[0, m] = jnp.where((named_t > 0.0) & (slot_t < CAP), part_row * CAP + slot_t, -1.0)
+        pos_tok[m] = jnp.where((named > 0.0) & (slot < CAP), part_col * CAP + slot, -1.0)
+
+    def place(which, m):
+        pos = post[which, m]
+        four = jnp.concatenate([pos] * BLOCKS, axis=1)
+        plain = count((ROWS, tok), 0).astype(F32)
+        down, across = count((ROWS, BLOCKS * tok), 0), count((ROWS, BLOCKS * tok), 1)
+        shift = tok.bit_length() - 1
+        own = lax.shift_right_logical(across, shift) == lax.shift_right_logical(down, 2)
+        slot = jnp.where(own, (ROWS + (down & 3)).astype(F32), -2.0)
+        for e in range(experts):
+            rows = pl.ds(e * ROWS, ROWS)
+            pm_ref[which, m, rows, :] = jnp.where(pos[e : e + 1] == plain, 1.0, 0.0).astype(BF16)
+            pe_ref[which, m, rows, :] = jnp.where(four[e : e + 1] == slot, 1.0, 0.0).astype(BF16)
+
+    def gather(m):
+        lanes = experts * ROWS
+        e_across = count((tok, experts), 1)
+        ids, wt = ids_ref[m], wt_ref[m]
+        weight = jnp.where(ids[:, 0:1] == e_across, wt[:, 0:1], 0.0)
+        weight = weight + jnp.where(ids[:, 1:2] == e_across, wt[:, 1:2], 0.0)
+        high = weight.astype(BF16)
+        low = (weight - high.astype(F32)).astype(BF16)
+        block = lax.shift_right_logical(count((experts, lanes), 1), 4) == count((experts, lanes), 0)
+        widen = jnp.where(block, 1.0, 0.0).astype(BF16)
+        pos = dot(pos_tok[m].astype(BF16), widen)
+        lane = count((tok, lanes), 1)
+        inside = lane & (ROWS - 1)
+        plain = inside.astype(F32)
+        tail = (ROWS + (lane & 3)).astype(F32)
+        for n, half in enumerate((high, low)):
+            value = dot(half, widen)
+            cm_ref[m, pl.ds(n * tok, tok), :] = jnp.where(pos == plain, value, 0.0).astype(BF16)
+            for b in range(BLOCKS):
+                mine = (pos == tail) & (lax.shift_right_logical(inside, 2) == b)
+                ce_ref[m, pl.ds((n * BLOCKS + b) * tok, tok), :] = jnp.where(mine, value, 0.0).astype(BF16)
+
+    for m in range(micro):
+        slots(m)
 
     barrier = pltpu.get_barrier_semaphore()
     for i in range(1, ranks):
@@ -152,6 +225,9 @@
             {"pipe": p + 1, "expert": e},
         )
 
+    def post_copy():
+        return remote(post.at[0], post.at[1], post_send, post_recv, {"pipe": p - 1})
+
     def stream_copy(m):
         return remote(out_ref.at[m], h_buf.at[m], h_send.at[m], h_recv.at[m], {"pipe": p + 1})
 
@@ -170,20 +246,10 @@
         g = j * sets + lax.rem(c, sets)
         return remote(back_out.at[c, j], back_in.at[m, me], b2_send.at[c, j], b2_recv.at[m, me], {"expert": g})
 
-    @pl.when(p == 0)
-    def _():
-        tok_load.wait()
-        for m in range(micro):
-            fill_messages(first_msg, 0, m, h_buf[m])
-            for i in range(1, experts):
-                first_copy(m, i).start()
-            x_buf[m * sets + my_set, t, my_place] = first_msg[m, me]
-
-    for load in loads:
-        load.wait()
-
     def relay(c):
-        for j in range(group):
+        near = lax.rem((me + experts - lax.rem(c, sets)) // 2, experts // 2) * 2 // sets
+        for n in range(group):
+            j = lax.rem(near + n, group)
             g = j * sets + lax.rem(c, sets)
 
             @pl.when((p > 0) | (g != me))
@@ -228,10 +294,14 @@
         act = (gate / (1.0 + jnp.exp(-gate)) * up).astype(BF16)
         for i in (2, 1, 3, 0):
             part = dot(act, w2[peer(i)]).astype(BF16)
+            extra = part[main_rows:]
+            stacked = jnp.concatenate([extra[:, b * narrow : (b + 1) * narrow] for b in range(BLOCKS)], axis=0)
+            packed = dot(pit_ref[...], stacked).astype(BF16)
+            wide = jnp.concatenate([part[:main_rows], packed], axis=1).reshape(group, ROWS, width + narrow)
             if i == 0:
-                part_in[c, t] = part
+                part_in[c, t] = wide
             else:
-                part_out[c, i - 1] = part
+                part_out[c, i - 1] = wide
                 part_copy(c, i).start()
 
     def give_back(c):
@@ -242,13 +312,7 @@
         total = part_in[c, 0].astype(F32)
         for q in range(1, ranks):
             total = total + part_in[c, q].astype(F32)
-        total = total.astype(BF16)
-        extra = total[main_rows:]
-        stacked = jnp.concatenate([extra[:, b * narrow : (b + 1) * narrow] for b in range(BLOCKS)], axis=0)
-        packed = dot(pit_ref[...], stacked).astype(BF16)
-        for j in range(group):
-            back_out[c, j, :, pl.ds(0, width)] = total[j * ROWS : (j + 1) * ROWS]
-            back_out[c, j, :, pl.ds(width, narrow)] = packed[j * ROWS : (j + 1) * ROWS]
+        back_out[c] = total.astype(BF16)
         for j in range(group):
             g = j * sets + lax.rem(c, sets)
 
@@ -286,12 +350,39 @@
             @pl.when(p < stages - 1)
             def _():
                 fill_messages(next_msg, 1, m, fresh)
-                for e in range(experts):
-                    next_copy(m, e).start()
+                for i in order:
+                    next_copy(m, other_chip(i)).start()
                 stream_copy(m).start()
 
+    @pl.when(p > 0)
+    def _():
+        post_copy().start()
+
+    @pl.when(p == 0)
+    def _():
+        tok_load.wait()
+        for m in range(micro):
+            place(0, m)
+            fill_messages(first_msg, 0, m, h_buf[m])
+            for i in range(1, experts):
+                first_copy(m, i).start()
+            x_buf[m * sets + my_set, t, my_place] = first_msg[m, me]
+        relay(0)
+
+    for m in range(micro):
+        gather(m)
+
+    @pl.when(p < stages - 1)
+    def _():
+        remote(post.at[0], post.at[1], post_send, post_recv, {"expert": other(1)}).wait_recv()
+        for m in range(micro):
+            place(1, m)
+
+    for load in loads:
+        load.wait()
+
     def step(s, carry):
-        @pl.when(s < chunks)
+        @pl.when((s < chunks) & ((s > 0) | (p > 0)))
         def _():
             relay(s)
 
@@ -310,6 +401,10 @@
         return carry
 
     lax.fori_loop(0, chunks + 1, step, 0)
+
+    @pl.when(p > 0)
+    def _():
+        post_copy().wait_send()
 
     @pl.when(p == 0)
     def _():
@@ -339,47 +434,6 @@
         return carry
 
     lax.fori_loop(0, chunks, drain, 0)
-
-
-def positions(ids, weights, order, experts, ranks):
-    tok = order.shape[-1]
-    index = jnp.arange(tok, dtype=jnp.int32)
-    rank = jnp.sum(jnp.where(order[:, :, None] == index[None, None, :], index[None, :, None], 0), axis=1)
-    quarter = rank // (tok // ranks)
-    names = ids[..., None] == jnp.arange(experts, dtype=jnp.int32)
-    named = jnp.any(names, axis=2)
-    weight = jnp.sum(jnp.where(names, weights[..., None], 0.0), axis=2)
-    before = (quarter[:, :, None] == quarter[:, None, :]) & (rank[:, None, :] < rank[:, :, None])
-    slot = jnp.sum((before[..., None] & named[:, None]).astype(jnp.int32), axis=2)
-    kept = named & (slot < CAP)
-    return jnp.where(kept, quarter[..., None] * CAP + slot, -1), weight
-
-
-def placing(pos):
-    micro, tok, experts = pos.shape
-    by_expert = jnp.swapaxes(pos, 1, 2)[:, :, None, :]
-    main = by_expert == jnp.arange(ROWS, dtype=jnp.int32)[None, None, :, None]
-    k = jnp.arange(BLOCKS, dtype=jnp.int32)
-    extra = by_expert[:, :, None, :, None, :] == (ROWS + k)[None, None, None, :, None, None]
-    same = k[:, None] == k[None, :]
-    extra = extra & same[None, None, :, None, :, None]
-    main = main.reshape(micro, experts * ROWS, tok).astype(BF16)
-    extra = extra.reshape(micro, experts * ROWS, BLOCKS * tok).astype(BF16)
-    return main, extra
-
-
-def gathering(pos, weight):
-    micro, tok, experts = pos.shape
-    high = weight.astype(BF16).astype(F32)
-    both = jnp.stack([high, weight - high], axis=1)[..., None]
-    main = jnp.where((pos[..., None] == jnp.arange(ROWS, dtype=jnp.int32))[:, None], both, 0.0)
-    k = jnp.arange(BLOCKS, dtype=jnp.int32)
-    extra = jnp.where((pos[..., None] == ROWS + k)[:, None], both, 0.0)
-    same = k[:, None] == k[None, :]
-    extra = jnp.where(same[None, None, :, None, None, :, None], extra[:, :, None, :, :, None, :], 0.0)
-    main = main.reshape(micro, 2 * tok, experts * ROWS).astype(BF16)
-    extra = extra.reshape(micro, 2 * BLOCKS * tok, experts * ROWS).astype(BF16)
-    return main, extra
 
 
 def local(sizes, tokens, gains, route_ids, route_weights, picks, w_gate, w_up, w_down):
@@ -394,13 +448,6 @@
     extra_rows = max(ROWS, BLOCKS * group)
     rows = main_rows + extra_rows
 
-    pos, weight = positions(route_ids[0], route_weights[0], picks[0, :, 0], experts, ranks)
-    following = lax.ppermute(pos, "pipe", [(i + 1, i) for i in range(stages - 1)])
-    pm, pe = placing(jnp.concatenate([pos, following], axis=0))
-    pm = pm.reshape(2, micro, *pm.shape[1:])
-    pe = pe.reshape(2, micro, *pe.shape[1:])
-    cm, ce = gathering(pos, weight)
-
     permute = np.zeros((BLOCKS, extra_rows, group, BLOCKS, BLOCKS), np.float32)
     for b in range(BLOCKS):
         for j in range(group):
@@ -416,16 +463,22 @@
     out = pl.pallas_call(
         functools.partial(kernel, sizes),
         out_shape=jax.ShapeDtypeStruct((micro, tok, width), BF16),
-        in_specs=[hbm] * 4 + [vmem] * 7,
+        in_specs=[hbm] * 4 + [vmem] * 8,
         out_specs=vmem,
         scratch_shapes=[
+            pltpu.VMEM((2, micro, experts * ROWS, tok), BF16),
+            pltpu.VMEM((2, micro, experts * ROWS, BLOCKS * tok), BF16),
+            pltpu.VMEM((micro, 2 * tok, experts * ROWS), BF16),
+            pltpu.VMEM((micro, 2 * BLOCKS * tok, experts * ROWS), BF16),
+            pltpu.VMEM((2, micro, experts, tok), F32),
+            pltpu.VMEM((micro, tok, experts), F32),
             pltpu.VMEM((ranks, width, 2 * hidden), BF16),
             pltpu.VMEM((ranks, hidden, width), BF16),
             pltpu.VMEM((chunks, ranks, group, ROWS, wide), BF16),
             pltpu.VMEM((ranks, rows, width), BF16),
             pltpu.VMEM((rows, 2 * hidden), F32),
-            pltpu.VMEM((chunks, ranks - 1, rows, width), BF16),
-            pltpu.VMEM((chunks, ranks, rows, width), BF16),
+            pltpu.VMEM((chunks, ranks - 1, group, ROWS, wide), BF16),
+            pltpu.VMEM((chunks, ranks, group, ROWS, wide), BF16),
             pltpu.VMEM((micro, experts, ROWS, wide), BF16),
             pltpu.VMEM((micro, experts, ROWS, wide), BF16),
             pltpu.VMEM((chunks, group, ROWS, wide), BF16),
@@ -443,6 +496,8 @@
             dma((micro, experts)),
             dma((micro,)),
             dma((micro,)),
+            dma,
+            dma,
         ],
         compiler_params=pltpu.CompilerParams(
             collective_id=0, has_side_effects=True, vmem_limit_bytes=60_000_000
@@ -453,10 +508,11 @@
         w_up[0, 0],
         w_down[0, 0],
         gains.reshape(ranks, 1, width),
-        pm,
-        pe,
-        cm,
-        ce,
+        route_ids[0],
+        jnp.swapaxes(route_ids[0], 1, 2),
+        route_weights[0],
+        picks[0],
+        jnp.swapaxes(picks[0], 1, 2),
         pi,
         pit,
     )

time: 316 us -> 293 us (0.927)
  Pallas kernels: 302 us -> 287 us
  other arithmetic: 7.26 us -> 0 us
    pallas_call x1, Pallas kernels: 302 us -> 287 us  [local(): pl.pallas_call(functools.partial(kernel, sizes), out_shape=jax.ShapeDtype...]
    reduce_sum x3 -> x0, other arithmetic: 3.72 us -> none  [the longest x1 2.24 us: positions(): jnp.sum((before[..., None] & named[:, None]).astype(jnp.int32), axis=2)]
  transfers between devices with their start and end apart: 1 -> 0, of which waited for: 0 -> 0; matrix products, arithmetic and copies ran while one was open for 1% -> 0% of each run, Pallas kernels for 0% -> 0%
where the time goes in v2:
time: 293 us
  Pallas kernels  287 us (98%)
  local copies, waits for them, and re-layouts  5.9 us (2%)
    pallas_call x1, Pallas kernels, local(): pl.pallas_call(functools.partial(kernel, sizes), out_shape=jax.ShapeDtype...  287 us

profile of v2, /device:TPU:103, one launch (start us, length us, event | category | flops | bytes accessed | tf_op | source)
XLA Modules:
  0.0 293.2 jit_solution(11540077124234201398)
XLA Ops:
  0.0 1.4 copy.11
  1.4 1.4 copy.14.col_ref
  2.8 1.4 copy.12.ids_ref
  4.2 287.3 %shard_map.100 = bf16[2,64,1024]{2,1,0:T(8,128)(2,1)} custom-call(bf16[2,64,4096]{2,1,0:T(8,128)(2,1)} %tok_hbm.1, bf16[4096,384]{1,0:T(8,128)(2,1)} %bitcast.13, bf16[4096,384]{1,0:T(8,128)(2,1)} %bitcast.14, bf16[384,4096]{1,0:T(8,128)(2,1)} %bitcast.15, f32[4,1,1024]{2,1,0:T(1,128)} %bitcast.18, s32[2,64,2]{2,1,0:T(8,128)} %copy.12.ids_ref, ...), custom_call_target="tpu_custom_call" | custom-call | tf_op jit(solution)/shard_map/pallas_call | solution.py:463
  291.5 1.7 copy.16

commit v3 on v2

--- a/solution.py
+++ b/solution.py
@@ -29,10 +29,8 @@
     wd_hbm,
     gain_ref,
     ids_ref,
-    idst_ref,
     wt_ref,
     row_ref,
-    col_ref,
     pi_ref,
     pit_ref,
     out_ref,
@@ -120,9 +118,13 @@
     def count(shape, dim):
         return lax.broadcasted_iota(jnp.int32, shape, dim)
 
+    def column(row):
+        mine = count((tok, tok), 0) == count((tok, tok), 1)
+        return jnp.sum(jnp.where(mine, row.astype(F32), 0.0), axis=1, keepdims=True)
+
     def slots(m):
         across, down = count((tok, tok), 1), count((tok, tok), 0)
-        rank_row = jnp.sum(jnp.where(col_ref[m] == across, down.astype(F32), 0.0), axis=0, keepdims=True)
+        rank_row = jnp.sum(jnp.where(column(row_ref[m]) == across.astype(F32), down.astype(F32), 0.0), axis=0, keepdims=True)
         rank_col = jnp.sum(jnp.where(row_ref[m] == down, across.astype(F32), 0.0), axis=1, keepdims=True)
         part_row = jnp.floor(rank_row * (ranks / tok))
         part_col = jnp.floor(rank_col * (ranks / tok))
@@ -130,9 +132,11 @@
         before_t = (jnp.where(rank_col < rank_row, 1.0, 0.0) * same).astype(BF16)
         before = (jnp.where(rank_row < rank_col, 1.0, 0.0) * same).astype(BF16)
         e_down, e_across = count((experts, tok), 0), count((tok, experts), 1)
-        ids, idst = ids_ref[m], idst_ref[m]
-        named_t = jnp.where((idst[0:1] == e_down) | (idst[1:2] == e_down), 1.0, 0.0)
-        named = jnp.where((ids[:, 0:1] == e_across) | (ids[:, 1:2] == e_across), 1.0, 0.0)
+        ids = ids_ref[m]
+        named_t = jnp.where((ids[0:1] == e_down) | (ids[1:2] == e_down), 1.0, 0.0)
+        first, second = column(ids[0:1]), column(ids[1:2])
+        e_across = e_across.astype(F32)
+        named = jnp.where((first == e_across) | (second == e_across), 1.0, 0.0)
         slot_t = dot(named_t.astype(BF16), before_t)
         slot = dot(before, named.astype(BF16))
         post[0, m] = jnp.where((named_t > 0.0) & (slot_t < CAP), part_row * CAP + slot_t, -1.0)
@@ -153,10 +157,10 @@
 
     def gather(m):
         lanes = experts * ROWS
-        e_across = count((tok, experts), 1)
+        e_across = count((tok, experts), 1).astype(F32)
         ids, wt = ids_ref[m], wt_ref[m]
-        weight = jnp.where(ids[:, 0:1] == e_across, wt[:, 0:1], 0.0)
-        weight = weight + jnp.where(ids[:, 1:2] == e_across, wt[:, 1:2], 0.0)
+        weight = jnp.where(column(ids[0:1]) == e_across, column(wt[0:1]), 0.0)
+        weight = weight + jnp.where(column(ids[1:2]) == e_across, column(wt[1:2]), 0.0)
         high = weight.astype(BF16)
         low = (weight - high.astype(F32)).astype(BF16)
         block = lax.shift_right_logical(count((experts, lanes), 1), 4) == count((experts, lanes), 0)
@@ -463,7 +467,7 @@
     out = pl.pallas_call(
         functools.partial(kernel, sizes),
         out_shape=jax.ShapeDtypeStruct((micro, tok, width), BF16),
-        in_specs=[hbm] * 4 + [vmem] * 8,
+        in_specs=[hbm] * 4 + [vmem] * 6,
         out_specs=vmem,
         scratch_shapes=[
             pltpu.VMEM((2, micro, experts * ROWS, tok), BF16),
@@ -508,11 +512,9 @@
         w_up[0, 0],
         w_down[0, 0],
         gains.reshape(ranks, 1, width),
-        route_ids[0],
         jnp.swapaxes(route_ids[0], 1, 2),
-        route_weights[0],
+        jnp.swapaxes(route_weights[0], 1, 2),
         picks[0],
-        jnp.swapaxes(picks[0], 1, 2),
         pi,
         pit,
     )

time: 293 us -> 289 us (0.986)
  local copies, waits for them, and re-layouts: 5.9 us -> 1.67 us
where the time goes in v3:
time: 289 us; the launch traced here: 288 us
  Pallas kernels  287 us (99%)
    pallas_call x1, Pallas kernels, local(): pl.pallas_call(functools.partial(kernel, sizes), out_shape=jax.ShapeDtype...  287 us

profile of v3, /device:TPU:103, one launch (start us, length us, event | category | flops | bytes accessed | tf_op | source)
XLA Modules:
  0.0 288.4 jit_solution(8883360930165536077)
XLA Ops:
  0.0 286.7 %shard_map.100 = bf16[2,64,1024]{2,1,0:T(8,128)(2,1)} custom-call(bf16[2,64,4096]{2,1,0:T(8,128)(2,1)} %tok_hbm.1, bf16[4096,384]{1,0:T(8,128)(2,1)} %bitcast.14, bf16[4096,384]{1,0:T(8,128)(2,1)} %bitcast.15, bf16[384,4096]{1,0:T(8,128)(2,1)} %bitcast.16, f32[4,1,1024]{2,1,0:T(1,128)} %bitcast.18, s32[2,2,64]{2,1,0:T(2,128)} %bitcast.19, ...), custom_call_target="tpu_custom_call" | custom-call | tf_op jit(solution)/shard_map/pallas_call | solution.py:467
  286.7 1.7 copy.13

commit v4 on v3

--- a/solution.py
+++ b/solution.py
@@ -362,16 +362,21 @@
     def _():
         post_copy().start()
 
+    def start(m):
+        fill_messages(first_msg, 0, m, h_buf[m])
+        for i in sorted(range(1, experts), key=lambda i: abs(2 * i - experts)):
+            first_copy(m, i).start()
+        x_buf[m * sets + my_set, t, my_place] = first_msg[m, me]
+
     @pl.when(p == 0)
     def _():
         tok_load.wait()
         for m in range(micro):
             place(0, m)
-            fill_messages(first_msg, 0, m, h_buf[m])
-            for i in range(1, experts):
-                first_copy(m, i).start()
-            x_buf[m * sets + my_set, t, my_place] = first_msg[m, me]
-        relay(0)
+
+        @pl.when(my_set == 0)
+        def _():
+            start(0)
 
     for m in range(micro):
         gather(m)
@@ -382,11 +387,20 @@
         for m in range(micro):
             place(1, m)
 
+    @pl.when(p == 0)
+    def _():
+        @pl.when(my_set > 0)
+        def _():
+            start(0)
+
+        for m in range(1, micro):
+            start(m)
+
     for load in loads:
         load.wait()
 
     def step(s, carry):
-        @pl.when((s < chunks) & ((s > 0) | (p > 0)))
+        @pl.when(s < chunks)
         def _():
             relay(s)
 

time: 289 us -> 286 us (0.990)
  Pallas kernels: 287 us -> 284 us
where the time goes in v4:
time: 286 us
  Pallas kernels  284 us (99%)
    pallas_call x1, Pallas kernels, local(): pl.pallas_call(functools.partial(kernel, sizes), out_shape=jax.ShapeDtype...  284 us

profile of v4, /device:TPU:103, one launch (start us, length us, event | category | flops | bytes accessed | tf_op | source)
XLA Modules:
  0.0 285.9 jit_solution(8658572313188358374)
XLA Ops:
  0.0 284.2 %shard_map.100 = bf16[2,64,1024]{2,1,0:T(8,128)(2,1)} custom-call(bf16[2,64,4096]{2,1,0:T(8,128)(2,1)} %tok_hbm.1, bf16[4096,384]{1,0:T(8,128)(2,1)} %bitcast.14, bf16[4096,384]{1,0:T(8,128)(2,1)} %bitcast.15, bf16[384,4096]{1,0:T(8,128)(2,1)} %bitcast.16, f32[4,1,1024]{2,1,0:T(1,128)} %bitcast.18, s32[2,2,64]{2,1,0:T(2,128)} %bitcast.19, ...), custom_call_target="tpu_custom_call" | custom-call | tf_op jit(solution)/shard_map/pallas_call | solution.py:481
  284.2 1.7 copy.13

commit v5 on v4

--- a/solution.py
+++ b/solution.py
@@ -262,7 +262,7 @@
                     first_msg.at[0, 0], x_buf.at[c, t, j], a1_send.at[0, 0, 0], a1_recv.at[c, j], {"expert": other(1)}
                 ).wait_recv()
 
-            for i in (2, 1, 3):
+            for i in (1, 3, 2):
                 relay_copy(c, j, i).start()
 
     def experts_work(c):

time: 286 us -> 281 us (0.983)
  Pallas kernels: 284 us -> 279 us
    pallas_call x1, Pallas kernels: 284 us -> 279 us  [local(): pl.pallas_call(functools.partial(kernel, sizes), out_shape=jax.ShapeDtype...]
where the time goes in v5:
time: 281 us
  Pallas kernels  279 us (99%)
    pallas_call x1, Pallas kernels, local(): pl.pallas_call(functools.partial(kernel, sizes), out_shape=jax.ShapeDtype...  279 us

profile of v5, /device:TPU:103, one launch (start us, length us, event | category | flops | bytes accessed | tf_op | source)
XLA Modules:
  0.0 280.9 jit_solution(18427519842398299093)
XLA Ops:
  0.0 279.2 %shard_map.100 = bf16[2,64,1024]{2,1,0:T(8,128)(2,1)} custom-call(bf16[2,64,4096]{2,1,0:T(8,128)(2,1)} %tok_hbm.1, bf16[4096,384]{1,0:T(8,128)(2,1)} %bitcast.14, bf16[4096,384]{1,0:T(8,128)(2,1)} %bitcast.15, bf16[384,4096]{1,0:T(8,128)(2,1)} %bitcast.16, f32[4,1,1024]{2,1,0:T(1,128)} %bitcast.18, s32[2,2,64]{2,1,0:T(2,128)} %bitcast.19, ...), custom_call_target="tpu_custom_call" | custom-call | tf_op jit(solution)/shard_map/pallas_call | solution.py:481
  279.2 1.7 copy.13

commit v6 on v5

--- a/solution.py
+++ b/solution.py
@@ -296,7 +296,7 @@
         gate = acc[:, pl.ds(0, hidden)] * inv
         up = acc[:, pl.ds(hidden, hidden)] * inv
         act = (gate / (1.0 + jnp.exp(-gate)) * up).astype(BF16)
-        for i in (2, 1, 3, 0):
+        for i in (1, 3, 2, 0):
             part = dot(act, w2[peer(i)]).astype(BF16)
             extra = part[main_rows:]
             stacked = jnp.concatenate([extra[:, b * narrow : (b + 1) * narrow] for b in range(BLOCKS)], axis=0)

time: 281 us -> 288 us (1.025)
  Pallas kernels: 279 us -> 286 us
    pallas_call x1, Pallas kernels: 279 us -> 286 us  [local(): pl.pallas_call(functools.partial(kernel, sizes), out_shape=jax.ShapeDtype...]
where the time goes in v6:
time: 288 us
  Pallas kernels  286 us (99%)
    pallas_call x1, Pallas kernels, local(): pl.pallas_call(functools.partial(kernel, sizes), out_shape=jax.ShapeDtype...  286 us

profile of v6, /device:TPU:103, one launch (start us, length us, event | category | flops | bytes accessed | tf_op | source)
XLA Modules:
  0.0 287.7 jit_solution(14325650676178133766)
XLA Ops:
  0.0 286.1 %shard_map.100 = bf16[2,64,1024]{2,1,0:T(8,128)(2,1)} custom-call(bf16[2,64,4096]{2,1,0:T(8,128)(2,1)} %tok_hbm.1, bf16[4096,384]{1,0:T(8,128)(2,1)} %bitcast.14, bf16[4096,384]{1,0:T(8,128)(2,1)} %bitcast.15, bf16[384,4096]{1,0:T(8,128)(2,1)} %bitcast.16, f32[4,1,1024]{2,1,0:T(1,128)} %bitcast.18, s32[2,2,64]{2,1,0:T(2,128)} %bitcast.19, ...), custom_call_target="tpu_custom_call" | custom-call | tf_op jit(solution)/shard_map/pallas_call | solution.py:481
  286.1 1.7 copy.13
